TPU v7x, 8 devices: a whole 2x2x1 slice. The times are simulated.
8 devices in a mesh: data: 2 (over z, y), seq: 4 (over x, core).
Axes of the slice: x: 2, y: 2, z: 1, core: 2. Of those that a mesh axis runs over, the one named last changes fastest.
Arguments:
- tokens: bfloat16 [8, 1024, 384], P('data', 'seq'), parts along dimension 0
- lengths: int32 [8], P('data'), parts along dimension 0
- slot_param: bfloat16 [384, 4096], replicated
- logit_scale: float32 [], replicated
- w_in: bfloat16 [256, 384, 1536], P('seq')
- w_out: bfloat16 [256, 1536, 384], P('seq')
Outputs:
- output: bfloat16 [8, 1024, 384], P('data', 'seq'), parts along dimension 0
There are 2 independent parts. A program takes and returns all parts, laid end to end along the dimension named above; an argument that names none is the same for every part.
All inputs are finite; a program needn't handle non-finite values.
Results may differ from a plain program's by a relative error of at most 0.0138026.
Values are sent between devices in bfloat16 or wider.
A program may use at most 1 GiB of HBM per device.

v0:
```python
import functools
import math

import jax
import jax.numpy as jnp
from jax import lax
from jax.experimental import pallas as pl
from jax.experimental.pallas import tpu as pltpu
from jax.sharding import PartitionSpec as P

EPSILON = 1e-6
NEG_FILL = -1e30
LOG2E = 1.0 / math.log(2.0)
F32 = jnp.float32
BF16 = jnp.bfloat16
RING = 14


def unit_rows(v32):
    return (v32 * lax.rsqrt(jnp.sum(v32 * v32, axis=1, keepdims=True) + EPSILON)).astype(BF16)


def gelu_tanh(h):
    inner = h * (math.sqrt(2.0 / math.pi) + (math.sqrt(2.0 / math.pi) * 0.044715) * (h * h))
    half = 0.5 * h
    return half + half * jnp.tanh(inner)


def row_of(col, rows):
    return jnp.broadcast_to(col, (rows, 128)).T[0:1, :]


def layer_kernel(
    scale_hbm, len_hbm, x_hbm, phi_hbm, w1_hbm, w2_hbm, out_ref,
    scale_ref, len_ref, xg, rm, rqs, rqr, wrow, ct, xs, d2r, hr, f1r, f2r, w1b, w2b,
    in_sem, w_sem, send_sem, r0_sem, r1_sem, rms_sem, rmr_sem, rqs_sem, rqr_sem, d2s_sem,
):
    nb, tok, dm = x_hbm.shape
    slots = xs.shape[1]
    n_slots = phi_hbm.shape[1]
    n_exp = slots // 16
    d = lax.axis_index("data")
    s = lax.axis_index("seq")
    xc, core = s // 2, s % 2
    to_p = {"data": d, "seq": 2 * xc + (1 - core)}
    to_x = {"data": d, "seq": 2 * (1 - xc) + core}
    to_y = {"data": 1 - d, "seq": s}

    def remote(src, dst, send, recv, dev):
        return pltpu.make_async_remote_copy(src_ref=src, dst_ref=dst, send_sem=send, recv_sem=recv, device_id=dev, device_id_type=pl.DeviceIdType.MESH)

    def weight_copies(e, slot):
        return (
            pltpu.make_async_copy(w1_hbm.at[n_exp * d + e], w1b.at[slot], w_sem.at[slot]),
            pltpu.make_async_copy(w2_hbm.at[n_exp * d + e], w2b.at[slot], w_sem.at[slot]),
        )

    barrier = pltpu.get_barrier_semaphore()
    for dev in (to_p, to_x, to_y):
        pl.semaphore_signal(barrier, inc=1, device_id=dev, device_id_type=pl.DeviceIdType.MESH)

    phi = ct.at[3, nb - 1, 0:dm]
    pnt = xs.at[2 * nb - 1]
    loads = [
        pltpu.make_async_copy(x_hbm, xg.at[0, :, 0], in_sem.at[0]),
        pltpu.make_async_copy(phi_hbm.at[:, pl.ds(pl.multiple_of(s * (n_slots // 4) + d * slots, slots), slots)], phi, in_sem.at[1]),
        pltpu.make_async_copy(len_hbm, len_ref, in_sem.at[2]),
        pltpu.make_async_copy(scale_hbm, scale_ref, in_sem.at[3]),
    ]
    for c in loads:
        c.start()

    by_x, by_y, by_p = send_sem.at[0], send_sem.at[1], send_sem.at[2]

    def blocks(ref, sem):
        return pltpu.make_async_copy(ref, ref, sem)

    def send_x(b):
        return remote(xg.at[0, b, 0], xg.at[1, b, 0], by_x, r0_sem.at[b], to_x)

    def send_y(b):
        return remote(xg.at[0, b, 0], xg.at[2, b, 0], by_y, r0_sem.at[b ^ 1], to_y)

    def send_p(b):
        return remote(xg.at[0, b, 0], xg.at[0, b, 1], by_p, r1_sem.at[b], to_p)

    half = tok // 2

    def fwd_across(r, b, h, send, dev):
        part = slice(h * half, (h + 1) * half)
        return remote(xg.at[r, b, 0, part], xg.at[3, b, 0, part], send, r0_sem.at[4 + 2 * (b // 2) + h], dev)

    def arrive_pair(j):
        other = j + 1 - 2 * (j % 2)
        blocks(xg.at[0, 0], r0_sem.at[j]).wait()
        for r, b in ((1, j), (2, other)):
            remote(xg.at[r, b, 0], xg.at[r, b, 1], by_p, r1_sem.at[nb + j], to_p).start()

        @pl.when(j % 2 == 0)
        def _():
            for h in range(2):
                fwd_across(1, j, h, by_y, to_y).start()
                fwd_across(2, other, h, by_x, to_x).start()

    def arrive_across(j, h):
        part = slice(h * half, (h + 1) * half)
        blocks(xg.at[0, 0, 0], r0_sem.at[4 + 2 * j + h]).wait()
        for b in (2 * j, 2 * j + 1):
            remote(xg.at[3, b, 0, part], xg.at[3, b, 1, part], by_p, r1_sem.at[2 * nb + j], to_p).start()

    rm_x = remote(rm.at[0, 0], rm.at[1, 0], rms_sem.at[0], rmr_sem.at[0], to_x)
    rm_y = remote(rm.at[0, 0], rm.at[2, 0], rms_sem.at[0], rmr_sem.at[0], to_y)
    rm_f = remote(rm.at[1, 0], rm.at[3, 0], rms_sem.at[0], rmr_sem.at[1], to_y)
    rm_p = [remote(rm.at[r, 0], rm.at[r, 1], rms_sem.at[1], rmr_sem.at[(2, 3, 3, 4)[r]], to_p) for r in range(4)]

    def phase_dispatch(acc, m_s, z_s):
        loads[2].wait()
        pos = s * tok + lax.broadcasted_iota(jnp.int32, (1, tok), 1)
        for b in range(nb):
            rm[0, 0, b:b + 1, :] = jnp.where(pos < len_ref[b], 0.0, NEG_FILL)
        loads[0].wait()
        pl.semaphore_wait(barrier, 3)
        rm_x.start()
        rm_y.start()
        rm_p[0].start()
        for b in range(nb):
            send_x(b).start()
            send_y(b ^ 1).start()
        for b in range(nb):
            send_p(b).start()
        for e in range(RING):
            for c in weight_copies(e, e):
                c.start()
        loads[3].wait()
        g2 = scale_ref[0] * LOG2E
        loads[1].wait()
        v = phi[...].astype(F32)
        pnt[...] = (v * lax.rsqrt(jnp.sum(v * v, axis=0, keepdims=True) + EPSILON)).T.astype(BF16)
        blocks(rm.at[0], rmr_sem.at[0]).wait()
        for c in (rm_f, rm_p[1], rm_p[2]):
            c.start()

        def unit(r, b, first, last):
            q = (r // 2) * nb + b
            a = b if r < 2 else b + 1 - 2 * (b % 2)
            xb = xg[r, b].reshape(2 * tok, dm)
            xn = unit_rows(xb.astype(F32))
            lt = lax.dot_general(pnt[...], xn, (((1,), (1,)), ((), ())), preferred_element_type=F32) * g2
            lm = lt + jnp.concatenate([rm[r, k, pl.ds(b, 1), :] for k in range(2)], axis=1)
            mx = jnp.broadcast_to(jnp.max(lm, axis=1, keepdims=True), (slots, 128))
            if not first:
                m_old = m_s[a]
                mx = jnp.maximum(mx, m_old)
            e = jnp.exp2(lm - jnp.concatenate([mx] * 4, axis=1))
            z = (e[:, 0:128] + e[:, 128:256]) + (e[:, 256:384] + e[:, 384:512])
            part = jnp.dot(e.astype(BF16), xb, preferred_element_type=F32)
            cmax = jnp.max(lt, axis=0, keepdims=True)
            c = jnp.exp2(lt - cmax)
            rqs[0, r, pl.ds(b, 1), :] = cmax
            rqs[0, r, pl.ds(nb + b, 1), :] = jnp.sum(c, axis=0, keepdims=True)
            ct[r, b] = c.astype(BF16)
            if not first:
                corr = jnp.exp2(m_old - mx)
                z = z + z_s[a] * corr
                part = part + acc[a] * jnp.concatenate([corr] * 3, axis=1)
            if last:
                inv = 1.0 / jnp.broadcast_to(jnp.sum(z, axis=1, keepdims=True), (slots, 128))
                xs[q] = (part * jnp.concatenate([inv] * 3, axis=1)).astype(BF16)
            else:
                m_s[a] = mx
                z_s[a] = z
                acc[a] = part

        blocks(rm.at[0, 0], rmr_sem.at[2]).wait()

        @pl.loop(0, nb)
        def _(b):
            blocks(xg.at[0, 0, 0], r1_sem.at[b]).wait()
            unit(0, b, True, False)

        arrive_pair(0)
        blocks(rm.at[0], rmr_sem.at[3]).wait()

        @pl.loop(0, nb)
        def _(j):
            blocks(xg.at[0, 0], r1_sem.at[nb + j]).wait()
            unit(1, j, False, True)

            @pl.when(j < nb - 1)
            def _():
                arrive_pair(j + 1)

            unit(2, j + 1 - 2 * (j % 2), True, False)

        blocks(rm.at[0, 0], rmr_sem.at[1]).wait()
        rm_p[3].start()
        for h in range(2):
            arrive_across(0, h)
        blocks(rm.at[0, 0], rmr_sem.at[4]).wait()

        @pl.loop(0, nb // 2)
        def _(j):
            blocks(xg.at[0, 0], r1_sem.at[2 * nb + j]).wait()
            unit(3, 2 * j, False, True)

            @pl.when(j < nb // 2 - 1)
            def _():
                arrive_across(j + 1, 0)

            unit(3, 2 * j + 1, False, True)

            @pl.when(j < nb // 2 - 1)
            def _():
                arrive_across(j + 1, 1)

        blocks(xg.at[0, 0:3], by_x).wait()
        blocks(xg.at[0, 0:3], by_y).wait()
        blocks(xg.at[0:2], by_p).wait()
        blocks(rm.at[0:3, 0], rms_sem.at[0]).wait()
        blocks(rm.at[0:2], rms_sem.at[1]).wait()

    pl.run_scoped(
        phase_dispatch,
        pltpu.VMEM((nb, slots, dm), F32),
        pltpu.VMEM((nb, slots, 128), F32),
        pltpu.VMEM((nb, slots, 128), F32),
    )

    rq_copies = [remote(rqs.at[k], rqr.at[k], rqs_sem.at[0], rqr_sem.at[k], dev) for k, dev in enumerate((to_p, to_x, to_y))]

    def merge(k):
        rq_copies[k].wait()
        for r in range(4):
            if k == 0:
                theirs = jnp.concatenate([rqr[k, r][:, tok:], rqr[k, r][:, :tok]], axis=1)
            else:
                theirs = rqr[k, r ^ k]
            mine = rqs[k, r]
            top = jnp.maximum(mine[:nb], theirs[:nb])
            low = mine[nb:] * jnp.exp2(mine[:nb] - top) + theirs[nb:] * jnp.exp2(theirs[:nb] - top)
            rqs[k + 1, r, :nb] = top
            rqs[k + 1, r, nb:] = low
            if k == 2:
                wrow[r] = jnp.exp2(rqs[0, r][:nb] - top)
        if k < 2:
            rq_copies[k + 1].start()

    rq_copies[0].start()

    def ffn(es):
        for e in es:
            blocks(w1b.at[0:2], w_sem.at[e % RING]).wait()
        rows = [pl.ds(pl.multiple_of(e * 16, 16), 16) for e in es]
        xe = [xs[:, r, :].reshape(2 * nb * 16, dm) for r in rows]
        hs = [jnp.dot(x, w1b[e % RING], preferred_element_type=F32) for x, e in zip(xe, es)]
        ys = [jnp.dot(gelu_tanh(h).astype(BF16), w2b[e % RING], preferred_element_type=F32) for h, e in zip(hs, es)]
        for y, r in zip(ys, rows):
            xs[:, r, :] = y.astype(BF16).reshape(2 * nb, 16, dm)
        for e in es:
            @pl.when(e + RING < n_exp)
            def _():
                for c in weight_copies(e + RING, e % RING):
                    c.start()

    ffn([0, 1])

    @pl.loop(0, (n_exp - 4) // 4)
    def _(i):
        ffn([4 * i + 2 + k for k in range(4)])
        for k in range(3):
            @pl.when(i == 2 * k + 1)
            def _():
                merge(k)

    ffn([n_exp - 2, n_exp - 1])

    def phase_combine(d2s, stash):
        def d2_start(r, b, g):
            remote(d2s.at[r, b], d2r.at[r, b], d2s_sem.at[g], r1_sem.at[g], to_p).start()

        def d2_wait(g, count):
            blocks(d2s.at[0, 0:count], d2s_sem.at[g]).wait()
            blocks(d2r.at[0, 0:count], r1_sem.at[g]).wait()

        def half_sum(r, b, cols):
            yt = xs[(r // 2) * nb + b].astype(F32).T.astype(BF16)
            return jnp.dot(yt, ct[r, b, :, cols], preferred_element_type=F32) * wrow[r, pl.ds(b, 1), :][:, cols]

        def comp(r, b, g):
            d2s[r, b] = half_sum(r, b, slice(tok, 2 * tok)).astype(BF16)
            d2_start(r, b, g)

        def mine(r, b):
            return half_sum(r, b, slice(0, tok))

        def h_start(b, odd):
            send, dev = (by_y, to_y) if odd else (by_x, to_x)
            remote(d2s.at[3, b], hr.at[b], send, r0_sem.at[b // 2], dev).start()

        def f1_start(b):
            remote(d2s.at[1, b], f1r.at[b], by_x, r0_sem.at[nb + b], to_x).start()

        def f2_start(b):
            remote(d2s.at[2, b], f2r.at[b], by_y, r0_sem.at[nb + b], to_y).start()

        @pl.loop(0, nb)
        def _(b):
            comp(3, b, b // 2)

        @pl.loop(0, nb // 2)
        def _(j):
            b0, b1 = 2 * j, 2 * j + 1
            t0 = mine(3, b0)
            d2_wait(j, 2)
            d2s[3, b0] = (t0 + d2r[3, b0].astype(F32)).astype(BF16)
            h_start(b0, False)
            d2s[3, b1] = (mine(3, b1) + d2r[3, b1].astype(F32)).astype(BF16)
            h_start(b1, True)
            comp(1, b0, 2 + j)
            comp(2, b1, 2 + j)

        @pl.loop(0, nb // 2)
        def _(j):
            b0, b1 = 2 * j, 2 * j + 1
            d2_wait(2 + j, 2)
            d2s[1, b0] = (mine(1, b0) + d2r[1, b0].astype(F32)).astype(BF16)
            f1_start(b0)
            d2s[2, b1] = (mine(2, b1) + d2r[2, b1].astype(F32)).astype(BF16)
            f2_start(b1)
            comp(1, b1, 4 + j)
            comp(2, b0, 4 + j)

        @pl.loop(0, nb // 2)
        def _(j):
            b0, b1 = 2 * j, 2 * j + 1
            t1, t2 = mine(1, b1), mine(2, b0)
            d2_wait(4 + j, 2)
            t1 += d2r[1, b1].astype(F32)
            t2 += d2r[2, b0].astype(F32)
            blocks(hr.at[0:2], r0_sem.at[j]).wait()
            d2s[1, b1] = (t1 + hr[b1].astype(F32)).astype(BF16)
            f1_start(b1)
            d2s[2, b0] = (t2 + hr[b0].astype(F32)).astype(BF16)
            f2_start(b0)

        @pl.loop(0, nb)
        def _(b):
            comp(0, b, 6)

        @pl.loop(0, nb)
        def _(b):
            stash[b] = mine(0, b)

        d2_wait(6, nb)

        @pl.loop(0, nb)
        def _(b):
            base = stash[b] + d2r[0, b].astype(F32)
            blocks(f1r.at[0:2], r0_sem.at[nb + b]).wait()
            pos = s * tok + lax.broadcasted_iota(jnp.int32, (1, tok), 1)
            y = (base + f1r[b].astype(F32) + f2r[b].astype(F32)) / rqs[3, 0, pl.ds(nb + b, 1), :tok]
            y = jnp.where(pos < len_ref[b], y, 0.0)
            out_ref[b] = y.T.astype(BF16)

        blocks(xg.at[0, 0:3], by_x).wait()
        blocks(xg.at[0, 0:3], by_y).wait()

    pl.run_scoped(
        phase_combine,
        pltpu.VMEM((4, nb, dm, tok), BF16),
        pltpu.VMEM((nb, dm, tok), F32),
    )


def solution(mesh):
    def local_layer(tok_blk, len_blk, slot_param, logit_scale, w_in, w_out):
        nb, tok, dm = tok_blk.shape
        n_slots = slot_param.shape[1]
        slots = n_slots // 8
        ff = w_in.shape[2]
        hbm = pl.BlockSpec(memory_space=pl.ANY)
        dma = pltpu.SemaphoreType.DMA
        return pl.pallas_call(
            layer_kernel,
            out_shape=pltpu.VMEM((nb, tok, dm), BF16),
            in_specs=[hbm] * 6,
            out_specs=pl.BlockSpec(memory_space=pltpu.VMEM),
            scratch_shapes=[
                pltpu.SMEM((1,), F32),
                pltpu.SMEM((nb,), jnp.int32),
                pltpu.VMEM((4, nb, 2, tok, dm), BF16),
                pltpu.VMEM((4, 2, nb, tok), F32),
                pltpu.VMEM((4, 4, 2 * nb, 2 * tok), F32),
                pltpu.VMEM((3, 4, 2 * nb, 2 * tok), F32),
                pltpu.VMEM((4, nb, 2 * tok), F32),
                pltpu.VMEM((4, nb, slots, 2 * tok), BF16),
                pltpu.VMEM((2 * nb, slots, dm), BF16),
                pltpu.VMEM((4, nb, dm, tok), BF16),
                pltpu.VMEM((nb, dm, tok), BF16),
                pltpu.VMEM((nb, dm, tok), BF16),
                pltpu.VMEM((nb, dm, tok), BF16),
                pltpu.VMEM((RING, dm, ff), BF16),
                pltpu.VMEM((RING, ff, dm), BF16),
                dma((4,)), dma((RING,)), dma((3,)), dma((2 * nb,)), dma((2 * nb + 2,)), dma((2,)), dma((5,)), dma((1,)), dma((3,)), dma((7,)),
            ],
            compiler_params=pltpu.CompilerParams(collective_id=0, has_side_effects=True, vmem_limit_bytes=66_250_000),
            name="soft_moe_layer",
        )(logit_scale.reshape(1), len_blk, tok_blk, slot_param, w_in, w_out)

    return jax.shard_map(local_layer, mesh=mesh, in_specs=(P("data", "seq", None), P("data"), P(None, None), P(), P("seq", None, None), P("seq", None, None)), out_specs=P("data", "seq", None), check_vma=False)
```

profile of v0, /device:TPU:0, one launch (start us, length us, event | category | flops | bytes accessed | tf_op | source)
XLA Modules:
  0.0 83.4 jit_solution(13292156147674476330)
XLA Ops:
  0.7 81.8 %soft_moe_layer.1 = bf16[4,256,384]{2,1,0:T(8,128)(2,1)S(1)} custom-call(f32[1]{0:T(128)} %bitcast.1.scale_hbm, s32[4]{0:T(128)} %len_hbm.1, bf16[4,256,384]{2,1,0:T(8,128)(2,1)} %x_hbm.1, bf16[384,4096]{1,0:T(8,128)(2,1)} %phi_hbm.1, bf16[64,384,1536]{2,1,0:T(8,128)(2,1)} %w1_hbm.1, bf16[64,1536,384]{2,1,0:T(8,128)(2,1)} %w2_hbm.1), custom_call_target="tpu_custom_call" | custom-call | tf_op jit(solution)/shard_map/soft_moe_layer/pallas_call | solution.py:383
  82.5 0.9 %copy.8 = bf16[4,256,384]{2,1,0:T(8,128)(2,1)} copy(bf16[4,256,384]{2,1,0:T(8,128)(2,1)S(1)} %soft_moe_layer.1) | data formatting | bytes 1572864
where the time goes:
time: 83.5 us; the launch traced here: 83.4 us
  Pallas kernels  81.8 us (98%)
  local copies, waits for them, and re-layouts  0.88 us (1%)
    pallas_call x1, Pallas kernels, local_layer(): pl.pallas_call(layer_kernel, out_shape=pltpu.VMEM((nb, tok, dm), BF16), i...  81.8 us

commit v1 on v0

--- a/solution.py
+++ b/solution.py
@@ -84,10 +84,10 @@
     def send_p(b):
         return remote(xg.at[0, b, 0], xg.at[0, b, 1], by_p, r1_sem.at[b], to_p)
 
-    half = tok // 2
+    cuts = (slice(0, tok // 2), slice(tok // 2, tok))
 
     def fwd_across(r, b, h, send, dev):
-        part = slice(h * half, (h + 1) * half)
+        part = cuts[h]
         return remote(xg.at[r, b, 0, part], xg.at[3, b, 0, part], send, r0_sem.at[4 + 2 * (b // 2) + h], dev)
 
     def arrive_pair(j):
@@ -103,8 +103,8 @@
                 fwd_across(2, other, h, by_x, to_x).start()
 
     def arrive_across(j, h):
-        part = slice(h * half, (h + 1) * half)
-        blocks(xg.at[0, 0, 0], r0_sem.at[4 + 2 * j + h]).wait()
+        part = cuts[h]
+        blocks(xg.at[0, 0, :, part], r0_sem.at[4 + 2 * j + h]).wait()
         for b in (2 * j, 2 * j + 1):
             remote(xg.at[3, b, 0, part], xg.at[3, b, 1, part], by_p, r1_sem.at[2 * nb + j], to_p).start()
 
@@ -190,28 +190,32 @@
             def _():
                 arrive_pair(j + 1)
 
+            @pl.when(j == nb - 1)
+            def _():
+                blocks(rm.at[0, 0], rmr_sem.at[1]).wait()
+                rm_p[3].start()
+                arrive_across(0, 0)
+
             unit(2, j + 1 - 2 * (j % 2), True, False)
 
-        blocks(rm.at[0, 0], rmr_sem.at[1]).wait()
-        rm_p[3].start()
-        for h in range(2):
-            arrive_across(0, h)
+        arrive_across(0, 1)
         blocks(rm.at[0, 0], rmr_sem.at[4]).wait()
 
-        @pl.loop(0, nb // 2)
-        def _(j):
-            blocks(xg.at[0, 0], r1_sem.at[2 * nb + j]).wait()
-            unit(3, 2 * j, False, True)
-
-            @pl.when(j < nb // 2 - 1)
-            def _():
-                arrive_across(j + 1, 0)
-
-            unit(3, 2 * j + 1, False, True)
-
-            @pl.when(j < nb // 2 - 1)
-            def _():
-                arrive_across(j + 1, 1)
+        blocks(xg.at[0, 0], r1_sem.at[2 * nb]).wait()
+
+        @pl.loop(0, 2)
+        def _(b):
+            unit(3, b, False, True)
+            for h in range(2):
+                @pl.when(b == h)
+                def _():
+                    arrive_across(1, h)
+
+        blocks(xg.at[0, 0], r1_sem.at[2 * nb + 1]).wait()
+
+        @pl.loop(2, nb)
+        def _(b):
+            unit(3, b, False, True)
 
         blocks(xg.at[0, 0:3], by_x).wait()
         blocks(xg.at[0, 0:3], by_y).wait()
@@ -264,7 +268,7 @@
 
     ffn([0, 1])
 
-    @pl.loop(0, (n_exp - 4) // 4)
+    @pl.loop(0, (n_exp - 8) // 4)
     def _(i):
         ffn([4 * i + 2 + k for k in range(4)])
         for k in range(3):
@@ -272,7 +276,9 @@
             def _():
                 merge(k)
 
-    ffn([n_exp - 2, n_exp - 1])
+    @pl.loop(0, 3)
+    def _(i):
+        ffn([n_exp - 6 + 2 * i, n_exp - 5 + 2 * i])
 
     def phase_combine(d2s, stash):
         def d2_start(r, b, g):
@@ -303,21 +309,35 @@
         def f2_start(b):
             remote(d2s.at[2, b], f2r.at[b], by_y, r0_sem.at[nb + b], to_y).start()
 
-        @pl.loop(0, nb)
-        def _(b):
-            comp(3, b, b // 2)
-
-        @pl.loop(0, nb // 2)
-        def _(j):
-            b0, b1 = 2 * j, 2 * j + 1
-            t0 = mine(3, b0)
-            d2_wait(j, 2)
-            d2s[3, b0] = (t0 + d2r[3, b0].astype(F32)).astype(BF16)
-            h_start(b0, False)
-            d2s[3, b1] = (mine(3, b1) + d2r[3, b1].astype(F32)).astype(BF16)
-            h_start(b1, True)
-            comp(1, b0, 2 + j)
-            comp(2, b1, 2 + j)
+        @pl.loop(0, 2)
+        def _(b):
+            comp(3, b, b)
+
+        @pl.loop(0, 2)
+        def _(b):
+            stash[b] = mine(3, b)
+
+        for b in (0, 1):
+            d2_wait(b, 1)
+            d2s[3, b] = (stash[b] + d2r[3, b].astype(F32)).astype(BF16)
+            h_start(b, b == 1)
+
+        @pl.loop(2, 4)
+        def _(b):
+            comp(3, b, 7)
+
+        @pl.loop(2, 4)
+        def _(b):
+            stash[b] = mine(3, b)
+
+        comp(1, 0, 2)
+        comp(2, 1, 2)
+        d2_wait(7, 2)
+        for b in (2, 3):
+            d2s[3, b] = (stash[b] + d2r[3, b].astype(F32)).astype(BF16)
+            h_start(b, b == 3)
+        comp(1, 2, 3)
+        comp(2, 3, 3)
 
         @pl.loop(0, nb // 2)
         def _(j):
@@ -401,7 +421,7 @@
                 pltpu.VMEM((nb, dm, tok), BF16),
                 pltpu.VMEM((RING, dm, ff), BF16),
                 pltpu.VMEM((RING, ff, dm), BF16),
-                dma((4,)), dma((RING,)), dma((3,)), dma((2 * nb,)), dma((2 * nb + 2,)), dma((2,)), dma((5,)), dma((1,)), dma((3,)), dma((7,)),
+                dma((4,)), dma((RING,)), dma((3,)), dma((2 * nb,)), dma((2 * nb + 2,)), dma((2,)), dma((5,)), dma((1,)), dma((3,)), dma((8,)),
             ],
             compiler_params=pltpu.CompilerParams(collective_id=0, has_side_effects=True, vmem_limit_bytes=66_250_000),
             name="soft_moe_layer",

time: 83.5 us -> 82.6 us (0.989)
    pallas_call x1, Pallas kernels: 81.8 us -> 81 us  [local_layer(): pl.pallas_call(layer_kernel, out_shape=pltpu.VMEM((nb, tok, dm), BF16), i...]
where the time goes in v1:
time: 82.6 us; the launch traced here: 82.5 us
  Pallas kernels  81 us (98%)
  local copies, waits for them, and re-layouts  0.88 us (1%)
    pallas_call x1, Pallas kernels, local_layer(): pl.pallas_call(layer_kernel, out_shape=pltpu.VMEM((nb, tok, dm), BF16), i...  81 us

profile of v1, /device:TPU:0, one launch (start us, length us, event | category | flops | bytes accessed | tf_op | source)
XLA Modules:
  0.0 82.5 jit_solution(10619316262098131556)
XLA Ops:
  0.7 81.0 %soft_moe_layer.1 = bf16[4,256,384]{2,1,0:T(8,128)(2,1)S(1)} custom-call(f32[1]{0:T(128)} %bitcast.1.scale_hbm, s32[4]{0:T(128)} %len_hbm.1, bf16[4,256,384]{2,1,0:T(8,128)(2,1)} %x_hbm.1, bf16[384,4096]{1,0:T(8,128)(2,1)} %phi_hbm.1, bf16[64,384,1536]{2,1,0:T(8,128)(2,1)} %w1_hbm.1, bf16[64,1536,384]{2,1,0:T(8,128)(2,1)} %w2_hbm.1), custom_call_target="tpu_custom_call" | custom-call | tf_op jit(solution)/shard_map/soft_moe_layer/pallas_call | solution.py:403
  81.6 0.9 %copy.8 = bf16[4,256,384]{2,1,0:T(8,128)(2,1)} copy(bf16[4,256,384]{2,1,0:T(8,128)(2,1)S(1)} %soft_moe_layer.1) | data formatting | bytes 1572864

commit v2 on v1

--- a/solution.py
+++ b/solution.py
@@ -79,34 +79,24 @@
         return remote(xg.at[0, b, 0], xg.at[1, b, 0], by_x, r0_sem.at[b], to_x)
 
     def send_y(b):
-        return remote(xg.at[0, b, 0], xg.at[2, b, 0], by_y, r0_sem.at[b ^ 1], to_y)
+        return remote(xg.at[0, b, 0], xg.at[2, b, 0], by_y, r0_sem.at[b], to_y)
 
     def send_p(b):
         return remote(xg.at[0, b, 0], xg.at[0, b, 1], by_p, r1_sem.at[b], to_p)
 
-    cuts = (slice(0, tok // 2), slice(tok // 2, tok))
-
-    def fwd_across(r, b, h, send, dev):
-        part = cuts[h]
-        return remote(xg.at[r, b, 0, part], xg.at[3, b, 0, part], send, r0_sem.at[4 + 2 * (b // 2) + h], dev)
-
-    def arrive_pair(j):
-        other = j + 1 - 2 * (j % 2)
-        blocks(xg.at[0, 0], r0_sem.at[j]).wait()
-        for r, b in ((1, j), (2, other)):
-            remote(xg.at[r, b, 0], xg.at[r, b, 1], by_p, r1_sem.at[nb + j], to_p).start()
-
-        @pl.when(j % 2 == 0)
-        def _():
-            for h in range(2):
-                fwd_across(1, j, h, by_y, to_y).start()
-                fwd_across(2, other, h, by_x, to_x).start()
-
-    def arrive_across(j, h):
-        part = cuts[h]
-        blocks(xg.at[0, 0, :, part], r0_sem.at[4 + 2 * j + h]).wait()
-        for b in (2 * j, 2 * j + 1):
-            remote(xg.at[3, b, 0, part], xg.at[3, b, 1, part], by_p, r1_sem.at[2 * nb + j], to_p).start()
+    def fwd_across(r, b, part, send, dev):
+        remote(xg.at[r, b, 0, part], xg.at[3, b, 0, part], send, r0_sem.at[nb + b], dev).start()
+
+    def arrive_pair(b):
+        blocks(xg.at[0, 0], r0_sem.at[b]).wait()
+        for r in (1, 2):
+            remote(xg.at[r, b, 0], xg.at[r, b, 1], by_p, r1_sem.at[nb + b], to_p).start()
+        fwd_across(1, b, slice(0, tok // 2), by_y, to_y)
+        fwd_across(2, b, slice(tok // 2, tok), by_x, to_x)
+
+    def arrive_across(b):
+        blocks(xg.at[0, 0, 0], r0_sem.at[nb + b]).wait()
+        remote(xg.at[3, b, 0], xg.at[3, b, 1], by_p, r1_sem.at[2 * nb + b], to_p).start()
 
     rm_x = remote(rm.at[0, 0], rm.at[1, 0], rms_sem.at[0], rmr_sem.at[0], to_x)
     rm_y = remote(rm.at[0, 0], rm.at[2, 0], rms_sem.at[0], rmr_sem.at[0], to_y)
@@ -125,7 +115,7 @@
         rm_p[0].start()
         for b in range(nb):
             send_x(b).start()
-            send_y(b ^ 1).start()
+            send_y(b).start()
         for b in range(nb):
             send_p(b).start()
         for e in range(RING):
@@ -142,7 +132,7 @@
 
         def unit(r, b, first, last):
             q = (r // 2) * nb + b
-            a = b if r < 2 else b + 1 - 2 * (b % 2)
+            a = b
             xb = xg[r, b].reshape(2 * tok, dm)
             xn = unit_rows(xb.astype(F32))
             lt = lax.dot_general(pnt[...], xn, (((1,), (1,)), ((), ())), preferred_element_type=F32) * g2
@@ -194,27 +184,21 @@
             def _():
                 blocks(rm.at[0, 0], rmr_sem.at[1]).wait()
                 rm_p[3].start()
-                arrive_across(0, 0)
-
-            unit(2, j + 1 - 2 * (j % 2), True, False)
-
-        arrive_across(0, 1)
+                arrive_across(0)
+
+            unit(2, j, True, False)
+
+        arrive_across(1)
         blocks(rm.at[0, 0], rmr_sem.at[4]).wait()
 
-        blocks(xg.at[0, 0], r1_sem.at[2 * nb]).wait()
-
-        @pl.loop(0, 2)
-        def _(b):
-            unit(3, b, False, True)
-            for h in range(2):
-                @pl.when(b == h)
-                def _():
-                    arrive_across(1, h)
-
-        blocks(xg.at[0, 0], r1_sem.at[2 * nb + 1]).wait()
-
-        @pl.loop(2, nb)
-        def _(b):
+        @pl.loop(0, nb)
+        def _(b):
+            @pl.when(b == nb - 2)
+            def _():
+                arrive_across(nb - 2)
+                arrive_across(nb - 1)
+
+            blocks(xg.at[0, 0, 0], r1_sem.at[2 * nb + b]).wait()
             unit(3, b, False, True)
 
         blocks(xg.at[0, 0:3], by_x).wait()
@@ -421,7 +405,7 @@
                 pltpu.VMEM((nb, dm, tok), BF16),
                 pltpu.VMEM((RING, dm, ff), BF16),
                 pltpu.VMEM((RING, ff, dm), BF16),
-                dma((4,)), dma((RING,)), dma((3,)), dma((2 * nb,)), dma((2 * nb + 2,)), dma((2,)), dma((5,)), dma((1,)), dma((3,)), dma((8,)),
+                dma((4,)), dma((RING,)), dma((3,)), dma((2 * nb,)), dma((3 * nb,)), dma((2,)), dma((5,)), dma((1,)), dma((3,)), dma((8,)),
             ],
             compiler_params=pltpu.CompilerParams(collective_id=0, has_side_effects=True, vmem_limit_bytes=66_250_000),
             name="soft_moe_layer",

time: 82.6 us -> 81.4 us (0.985)
  Pallas kernels: 81 us -> 79.8 us
    pallas_call x1, Pallas kernels: 81 us -> 79.8 us  [local_layer(): pl.pallas_call(layer_kernel, out_shape=pltpu.VMEM((nb, tok, dm), BF16), i...]
where the time goes in v2:
time: 81.4 us; the launch traced here: 81.3 us
  Pallas kernels  79.8 us (98%)
  local copies, waits for them, and re-layouts  0.88 us (1%)
    pallas_call x1, Pallas kernels, local_layer(): pl.pallas_call(layer_kernel, out_shape=pltpu.VMEM((nb, tok, dm), BF16), i...  79.8 us

profile of v2, /device:TPU:0, one launch (start us, length us, event | category | flops | bytes accessed | tf_op | source)
XLA Modules:
  0.0 81.3 jit_solution(11925591256445081603)
XLA Ops:
  0.7 79.8 %soft_moe_layer.1 = bf16[4,256,384]{2,1,0:T(8,128)(2,1)S(1)} custom-call(f32[1]{0:T(128)} %bitcast.1.scale_hbm, s32[4]{0:T(128)} %len_hbm.1, bf16[4,256,384]{2,1,0:T(8,128)(2,1)} %x_hbm.1, bf16[384,4096]{1,0:T(8,128)(2,1)} %phi_hbm.1, bf16[64,384,1536]{2,1,0:T(8,128)(2,1)} %w1_hbm.1, bf16[64,1536,384]{2,1,0:T(8,128)(2,1)} %w2_hbm.1), custom_call_target="tpu_custom_call" | custom-call | tf_op jit(solution)/shard_map/soft_moe_layer/pallas_call | solution.py:387
  80.4 0.9 %copy.8 = bf16[4,256,384]{2,1,0:T(8,128)(2,1)} copy(bf16[4,256,384]{2,1,0:T(8,128)(2,1)S(1)} %soft_moe_layer.1) | data formatting | bytes 1572864

commit v3 on v2

--- a/solution.py
+++ b/solution.py
@@ -283,79 +283,64 @@
         def mine(r, b):
             return half_sum(r, b, slice(0, tok))
 
-        def h_start(b, odd):
-            send, dev = (by_y, to_y) if odd else (by_x, to_x)
-            remote(d2s.at[3, b], hr.at[b], send, r0_sem.at[b // 2], dev).start()
-
-        def f1_start(b):
+        cut = tok // 2
+
+        def h_start(b):
+            for cols, send, dev in ((slice(0, cut), by_x, to_x), (slice(cut, tok), by_y, to_y)):
+                remote(d2s.at[3, b, :, cols], hr.at[b, :, cols], send, r0_sem.at[b], dev).start()
+
+        def f_start(b):
             remote(d2s.at[1, b], f1r.at[b], by_x, r0_sem.at[nb + b], to_x).start()
-
-        def f2_start(b):
             remote(d2s.at[2, b], f2r.at[b], by_y, r0_sem.at[nb + b], to_y).start()
 
         @pl.loop(0, 2)
         def _(b):
             comp(3, b, b)
 
+        @pl.loop(0, nb)
+        def _(b):
+            t = mine(3, b)
+            d2_wait(b, 1)
+            d2s[3, b] = (t + d2r[3, b].astype(F32)).astype(BF16)
+            h_start(b)
+
+            @pl.when(b < nb - 2)
+            def _():
+                comp(3, b + 2, b + 2)
+
+        @pl.loop(0, nb)
+        def _(b):
+            comp(1, b, nb + b)
+            comp(2, b, nb + b)
+
+        def hop(b):
+            t1, t2 = mine(1, b), mine(2, b)
+            d2_wait(nb + b, 2)
+            t1 += d2r[1, b].astype(F32)
+            t2 += d2r[2, b].astype(F32)
+            blocks(hr.at[0], r0_sem.at[b]).wait()
+            h = hr[b].astype(F32)
+            d2s[1, b] = jnp.concatenate([t1[:, :cut], t1[:, cut:] + h[:, cut:]], axis=1).astype(BF16)
+            d2s[2, b] = jnp.concatenate([t2[:, :cut] + h[:, :cut], t2[:, cut:]], axis=1).astype(BF16)
+            f_start(b)
+
         @pl.loop(0, 2)
         def _(b):
-            stash[b] = mine(3, b)
-
-        for b in (0, 1):
-            d2_wait(b, 1)
-            d2s[3, b] = (stash[b] + d2r[3, b].astype(F32)).astype(BF16)
-            h_start(b, b == 1)
-
-        @pl.loop(2, 4)
-        def _(b):
-            comp(3, b, 7)
-
-        @pl.loop(2, 4)
-        def _(b):
-            stash[b] = mine(3, b)
-
-        comp(1, 0, 2)
-        comp(2, 1, 2)
-        d2_wait(7, 2)
-        for b in (2, 3):
-            d2s[3, b] = (stash[b] + d2r[3, b].astype(F32)).astype(BF16)
-            h_start(b, b == 3)
-        comp(1, 2, 3)
-        comp(2, 3, 3)
-
-        @pl.loop(0, nb // 2)
-        def _(j):
-            b0, b1 = 2 * j, 2 * j + 1
-            d2_wait(2 + j, 2)
-            d2s[1, b0] = (mine(1, b0) + d2r[1, b0].astype(F32)).astype(BF16)
-            f1_start(b0)
-            d2s[2, b1] = (mine(2, b1) + d2r[2, b1].astype(F32)).astype(BF16)
-            f2_start(b1)
-            comp(1, b1, 4 + j)
-            comp(2, b0, 4 + j)
-
-        @pl.loop(0, nb // 2)
-        def _(j):
-            b0, b1 = 2 * j, 2 * j + 1
-            t1, t2 = mine(1, b1), mine(2, b0)
-            d2_wait(4 + j, 2)
-            t1 += d2r[1, b1].astype(F32)
-            t2 += d2r[2, b0].astype(F32)
-            blocks(hr.at[0:2], r0_sem.at[j]).wait()
-            d2s[1, b1] = (t1 + hr[b1].astype(F32)).astype(BF16)
-            f1_start(b1)
-            d2s[2, b0] = (t2 + hr[b0].astype(F32)).astype(BF16)
-            f2_start(b0)
-
-        @pl.loop(0, nb)
-        def _(b):
-            comp(0, b, 6)
+            hop(b)
+
+        @pl.loop(0, nb)
+        def _(b):
+            comp(0, b, 2 * nb)
 
         @pl.loop(0, nb)
         def _(b):
             stash[b] = mine(0, b)
 
-        d2_wait(6, nb)
+        @pl.loop(2, nb)
+        def _(b):
+            hop(b)
+
+        d2_wait(2 * nb, nb)
 
         @pl.loop(0, nb)
         def _(b):
@@ -405,7 +390,7 @@
                 pltpu.VMEM((nb, dm, tok), BF16),
                 pltpu.VMEM((RING, dm, ff), BF16),
                 pltpu.VMEM((RING, ff, dm), BF16),
-                dma((4,)), dma((RING,)), dma((3,)), dma((2 * nb,)), dma((3 * nb,)), dma((2,)), dma((5,)), dma((1,)), dma((3,)), dma((8,)),
+                dma((4,)), dma((RING,)), dma((3,)), dma((2 * nb,)), dma((3 * nb,)), dma((2,)), dma((5,)), dma((1,)), dma((3,)), dma((2 * nb + 1,)),
             ],
             compiler_params=pltpu.CompilerParams(collective_id=0, has_side_effects=True, vmem_limit_bytes=66_250_000),
             name="soft_moe_layer",

time: 81.4 us -> 81 us (level)
  no operation moved by 1% of the time
where the time goes in v3:
time: 81 us; the launch traced here: 80.9 us
  Pallas kernels  79.3 us (98%)
  local copies, waits for them, and re-layouts  0.88 us (1%)
    pallas_call x1, Pallas kernels, local_layer(): pl.pallas_call(layer_kernel, out_shape=pltpu.VMEM((nb, tok, dm), BF16), i...  79.3 us

profile of v3, /device:TPU:0, one launch (start us, length us, event | category | flops | bytes accessed | tf_op | source)
XLA Modules:
  0.0 80.9 jit_solution(13850814629098988202)
XLA Ops:
  0.7 79.3 %soft_moe_layer.1 = bf16[4,256,384]{2,1,0:T(8,128)(2,1)S(1)} custom-call(f32[1]{0:T(128)} %bitcast.1.scale_hbm, s32[4]{0:T(128)} %len_hbm.1, bf16[4,256,384]{2,1,0:T(8,128)(2,1)} %x_hbm.1, bf16[384,4096]{1,0:T(8,128)(2,1)} %phi_hbm.1, bf16[64,384,1536]{2,1,0:T(8,128)(2,1)} %w1_hbm.1, bf16[64,1536,384]{2,1,0:T(8,128)(2,1)} %w2_hbm.1), custom_call_target="tpu_custom_call" | custom-call | tf_op jit(solution)/shard_map/soft_moe_layer/pallas_call | solution.py:372
  80.0 0.9 %copy.8 = bf16[4,256,384]{2,1,0:T(8,128)(2,1)} copy(bf16[4,256,384]{2,1,0:T(8,128)(2,1)S(1)} %soft_moe_layer.1) | data formatting | bytes 1572864

commit v4 on v3

--- a/solution.py
+++ b/solution.py
@@ -9,7 +9,7 @@
 from jax.sharding import PartitionSpec as P
 
 EPSILON = 1e-6
-NEG_FILL = -1e30
+TOP = 3.4028235e38
 LOG2E = 1.0 / math.log(2.0)
 F32 = jnp.float32
 BF16 = jnp.bfloat16
@@ -20,14 +20,14 @@
     return (v32 * lax.rsqrt(jnp.sum(v32 * v32, axis=1, keepdims=True) + EPSILON)).astype(BF16)
 
 
+def expd(a, b):
+    return jnp.exp2((a - b) * LOG2E)
+
+
 def gelu_tanh(h):
     inner = h * (math.sqrt(2.0 / math.pi) + (math.sqrt(2.0 / math.pi) * 0.044715) * (h * h))
     half = 0.5 * h
     return half + half * jnp.tanh(inner)
-
-
-def row_of(col, rows):
-    return jnp.broadcast_to(col, (rows, 128)).T[0:1, :]
 
 
 def layer_kernel(
@@ -107,7 +107,7 @@
         loads[2].wait()
         pos = s * tok + lax.broadcasted_iota(jnp.int32, (1, tok), 1)
         for b in range(nb):
-            rm[0, 0, b:b + 1, :] = jnp.where(pos < len_ref[b], 0.0, NEG_FILL)
+            rm[0, 0, b:b + 1, :] = jnp.where(pos < len_ref[b], TOP, -TOP)
         loads[0].wait()
         pl.semaphore_wait(barrier, 3)
         rm_x.start()
@@ -122,7 +122,7 @@
             for c in weight_copies(e, e):
                 c.start()
         loads[3].wait()
-        g2 = scale_ref[0] * LOG2E
+        g = scale_ref[0]
         loads[1].wait()
         v = phi[...].astype(F32)
         pnt[...] = (v * lax.rsqrt(jnp.sum(v * v, axis=0, keepdims=True) + EPSILON)).T.astype(BF16)
@@ -135,22 +135,22 @@
             a = b
             xb = xg[r, b].reshape(2 * tok, dm)
             xn = unit_rows(xb.astype(F32))
-            lt = lax.dot_general(pnt[...], xn, (((1,), (1,)), ((), ())), preferred_element_type=F32) * g2
-            lm = lt + jnp.concatenate([rm[r, k, pl.ds(b, 1), :] for k in range(2)], axis=1)
+            lt = lax.dot_general(pnt[...], xn, (((1,), (1,)), ((), ())), preferred_element_type=F32) * g
+            lm = jnp.minimum(lt, jnp.concatenate([rm[r, k, pl.ds(b, 1), :] for k in range(2)], axis=1))
             mx = jnp.broadcast_to(jnp.max(lm, axis=1, keepdims=True), (slots, 128))
             if not first:
                 m_old = m_s[a]
                 mx = jnp.maximum(mx, m_old)
-            e = jnp.exp2(lm - jnp.concatenate([mx] * 4, axis=1))
+            e = expd(lm, jnp.concatenate([mx] * 4, axis=1))
             z = (e[:, 0:128] + e[:, 128:256]) + (e[:, 256:384] + e[:, 384:512])
             part = jnp.dot(e.astype(BF16), xb, preferred_element_type=F32)
             cmax = jnp.max(lt, axis=0, keepdims=True)
-            c = jnp.exp2(lt - cmax)
+            c = expd(lt, cmax)
             rqs[0, r, pl.ds(b, 1), :] = cmax
             rqs[0, r, pl.ds(nb + b, 1), :] = jnp.sum(c, axis=0, keepdims=True)
             ct[r, b] = c.astype(BF16)
             if not first:
-                corr = jnp.exp2(m_old - mx)
+                corr = expd(m_old, mx)
                 z = z + z_s[a] * corr
                 part = part + acc[a] * jnp.concatenate([corr] * 3, axis=1)
             if last:
@@ -225,11 +225,11 @@
                 theirs = rqr[k, r ^ k]
             mine = rqs[k, r]
             top = jnp.maximum(mine[:nb], theirs[:nb])
-            low = mine[nb:] * jnp.exp2(mine[:nb] - top) + theirs[nb:] * jnp.exp2(theirs[:nb] - top)
+            low = mine[nb:] * expd(mine[:nb], top) + theirs[nb:] * expd(theirs[:nb], top)
             rqs[k + 1, r, :nb] = top
             rqs[k + 1, r, nb:] = low
             if k == 2:
-                wrow[r] = jnp.exp2(rqs[0, r][:nb] - top)
+                wrow[r] = expd(rqs[0, r][:nb], top)
         if k < 2:
             rq_copies[k + 1].start()
 

time: 81 us -> 81.2 us (level)
  no operation moved by 1% of the time
where the time goes in v4:
time: 81.2 us; the launch traced here: 81.1 us
  Pallas kernels  79.5 us (98%)
  local copies, waits for them, and re-layouts  0.88 us (1%)
    pallas_call x1, Pallas kernels, local_layer(): pl.pallas_call(layer_kernel, out_shape=pltpu.VMEM((nb, tok, dm), BF16), i...  79.5 us

profile of v4, /device:TPU:0, one launch (start us, length us, event | category | flops | bytes accessed | tf_op | source)
XLA Modules:
  0.0 81.1 jit_solution(16161908998610619750)
XLA Ops:
  0.7 79.5 %soft_moe_layer.1 = bf16[4,256,384]{2,1,0:T(8,128)(2,1)S(1)} custom-call(f32[1]{0:T(128)} %bitcast.1.scale_hbm, s32[4]{0:T(128)} %len_hbm.1, bf16[4,256,384]{2,1,0:T(8,128)(2,1)} %x_hbm.1, bf16[384,4096]{1,0:T(8,128)(2,1)} %phi_hbm.1, bf16[64,384,1536]{2,1,0:T(8,128)(2,1)} %w1_hbm.1, bf16[64,1536,384]{2,1,0:T(8,128)(2,1)} %w2_hbm.1), custom_call_target="tpu_custom_call" | custom-call | tf_op jit(solution)/shard_map/soft_moe_layer/pallas_call | solution.py:372
  80.2 0.9 %copy.8 = bf16[4,256,384]{2,1,0:T(8,128)(2,1)} copy(bf16[4,256,384]{2,1,0:T(8,128)(2,1)S(1)} %soft_moe_layer.1) | data formatting | bytes 1572864

commit v5 on v4

--- a/solution.py
+++ b/solution.py
@@ -273,7 +273,7 @@
             blocks(d2r.at[0, 0:count], r1_sem.at[g]).wait()
 
         def half_sum(r, b, cols):
-            yt = xs[(r // 2) * nb + b].astype(F32).T.astype(BF16)
+            yt = xs[(r // 2) * nb + b].T
             return jnp.dot(yt, ct[r, b, :, cols], preferred_element_type=F32) * wrow[r, pl.ds(b, 1), :][:, cols]
 
         def comp(r, b, g):
@@ -347,9 +347,9 @@
             base = stash[b] + d2r[0, b].astype(F32)
             blocks(f1r.at[0:2], r0_sem.at[nb + b]).wait()
             pos = s * tok + lax.broadcasted_iota(jnp.int32, (1, tok), 1)
-            y = (base + f1r[b].astype(F32) + f2r[b].astype(F32)) / rqs[3, 0, pl.ds(nb + b, 1), :tok]
+            y = (base + f1r[b].astype(F32) + f2r[b].astype(F32)) * (1.0 / rqs[3, 0, pl.ds(nb + b, 1), :tok])
             y = jnp.where(pos < len_ref[b], y, 0.0)
-            out_ref[b] = y.T.astype(BF16)
+            out_ref[b] = y.astype(BF16).T
 
         blocks(xg.at[0, 0:3], by_x).wait()
         blocks(xg.at[0, 0:3], by_y).wait()

time: 81.2 us -> 81.2 us (level)
  no operation moved by 1% of the time
where the time goes in v5:
time: 81.2 us; the launch traced here: 81 us
  Pallas kernels  79.5 us (98%)
  local copies, waits for them, and re-layouts  0.88 us (1%)
    pallas_call x1, Pallas kernels, local_layer(): pl.pallas_call(layer_kernel, out_shape=pltpu.VMEM((nb, tok, dm), BF16), i...  79.5 us

profile of v5, /device:TPU:0, one launch (start us, length us, event | category | flops | bytes accessed | tf_op | source)
XLA Modules:
  0.0 81.0 jit_solution(16811047773483433844)
XLA Ops:
  0.7 79.5 %soft_moe_layer.1 = bf16[4,256,384]{2,1,0:T(8,128)(2,1)S(1)} custom-call(f32[1]{0:T(128)} %bitcast.1.scale_hbm, s32[4]{0:T(128)} %len_hbm.1, bf16[4,256,384]{2,1,0:T(8,128)(2,1)} %x_hbm.1, bf16[384,4096]{1,0:T(8,128)(2,1)} %phi_hbm.1, bf16[64,384,1536]{2,1,0:T(8,128)(2,1)} %w1_hbm.1, bf16[64,1536,384]{2,1,0:T(8,128)(2,1)} %w2_hbm.1), custom_call_target="tpu_custom_call" | custom-call | tf_op jit(solution)/shard_map/soft_moe_layer/pallas_call | solution.py:372
  80.2 0.9 %copy.8 = bf16[4,256,384]{2,1,0:T(8,128)(2,1)} copy(bf16[4,256,384]{2,1,0:T(8,128)(2,1)S(1)} %soft_moe_layer.1) | data formatting | bytes 1572864
